TPU v7x, 32 devices: a whole 2x2x4 slice. The times are simulated.
32 devices in a mesh: stack: 2 (over y), date: 4 (over x, core), line: 4 (over z).
Axes of the slice: x: 2, y: 2, z: 4, core: 2. Of those that a mesh axis runs over, the one named last changes fastest.
Arguments:
- slc: float32 [4, 2, 512, 1280], P('date', None, 'stack', 'line'), parts along dimension 2, may hold values from -6 to 6
- band_start: int32 [4], replicated, may hold values from 0 to 640, as said below
- band_stop: int32 [4], replicated, may hold values from 640 to 1280, as said below
Outputs:
- interferogram: float32 [4, 2, 512, 256], P('date', None, 'stack', 'line'), parts along dimension 2
There are 2 independent parts, one for each index of `stack`. A program takes and returns all parts, laid end to end along the dimension named above; an argument that names none is the same for every part. Nothing has to cross between parts.
Inputs may be any that keep to these rules, and one draw needn't show every extreme that they name: For every pair, band_stop - band_start lies between 640 and 960; at least one pair keeps exactly 960 bins, and some pair keeps exactly 640 bins ending at 1280. `band_stop`: see band_start.
All inputs are finite; a program needn't handle non-finite values.
Results may differ from a plain program's by a relative error of at most 0.0001.
Values sent between devices are 32-bit elements; how exact they have to be, the bound alone decides.
A program may use at most 64 MiB of HBM per device.

v0:
```python
import functools

import jax
import jax.numpy as jnp
import numpy as np
from jax import lax
from jax.experimental import pallas as pl
from jax.experimental.pallas import tpu as pltpu
from jax.sharding import PartitionSpec as P

LOOKS = 5
LANES = 128
MESH = pl.DeviceIdType.MESH
CHUNK = 16
SMALL = 16


def layout(width):
    full = width // LANES * LANES
    tail = width - full
    assert 2 * tail in (0, LANES)
    comp = np.concatenate([np.zeros(full), np.ones(full), np.zeros(tail), np.ones(tail)])
    index = np.concatenate([np.arange(full), np.arange(full), np.arange(tail) + full, np.arange(tail) + full])
    return full, tail, comp.astype(np.int64), index.astype(np.int64)


def split(values):
    high = values.astype(jnp.bfloat16)
    return high, (values - high.astype(jnp.float32)).astype(jnp.bfloat16)


def tables(outer, width):
    full, tail, comp, index = layout(width)
    angle = 2.0 * np.pi / width * (index[:, None] * index[None, :] % width)
    c, s = np.cos(angle), np.sin(angle)
    same = comp[:, None] == comp[None, :]
    to_re = (comp[:, None] == 1) & (comp[None, :] == 0)
    dense = np.where(same, c, np.where(to_re, s, -s)).astype(np.float32)
    high = dense.astype(jnp.bfloat16)
    low = (dense - high.astype(np.float32)).astype(jnp.bfloat16)
    inner = np.stack([high, low])
    lines = outer * width
    turn = 2.0 * np.pi / lines * (np.arange(outer)[:, None] * index[None, :] % lines)
    along = np.cos(turn)
    across = np.where(comp[None, :] == 0, np.sin(turn), -np.sin(turn))
    twist = np.stack([along, across], axis=1).astype(np.float32)
    bins = (np.arange(outer)[:, None] + outer * index[None, :]).astype(np.int32)[:, None, :]
    samples = width // LOOKS
    target = index // LOOKS + samples * comp
    pool = (target[:, None] == np.arange(2 * samples)[None, :]).astype(jnp.bfloat16)
    return inner, twist, bins, pool


def chunk_sizes(columns):
    sizes, left = [], columns
    while left > CHUNK and left % SMALL == 0:
        sizes.append(CHUNK)
        left -= CHUNK
    if left % SMALL == 0:
        return sizes + [SMALL] * (left // SMALL)
    return sizes + [left]


class Row:
    def __init__(self, re, im, tail):
        self.re, self.im, self.tail = re, im, tail

    def __add__(self, other):
        return Row(self.re + other.re, self.im + other.im, None if self.tail is None else self.tail + other.tail)

    def __sub__(self, other):
        return Row(self.re - other.re, self.im - other.im, None if self.tail is None else self.tail - other.tail)

    def flat(self):
        parts = [self.re, self.im] + ([] if self.tail is None else [self.tail])
        return jnp.concatenate(parts, axis=-1)


def as_row(values, full, tail):
    return Row(
        values[:, :full],
        values[:, full : 2 * full],
        values[:, 2 * full :] if tail else None,
    )


def swapped(tail_values):
    return pltpu.roll(tail_values, LANES // 2, 1)


def first_half(tail_values):
    return lax.broadcasted_iota(jnp.int32, tail_values.shape, 1) < LANES // 2


def times_minus_i(row):
    tail = row.tail
    if tail is not None:
        turned = swapped(tail)
        tail = jnp.where(first_half(tail), turned, -turned)
    return Row(row.im, -row.re, tail)


def times_phase(row, c, s):
    tail = row.tail
    if tail is not None:
        turned = swapped(tail) * s
        tail = tail * c + jnp.where(first_half(tail), turned, -turned)
    return Row(row.re * c + row.im * s, row.im * c - row.re * s, tail)


def short_dft(rows):
    count = len(rows)
    if count == 1:
        return rows
    if count % 2:
        result = []
        for k in range(count):
            total = rows[0]
            for n in range(1, count):
                angle = 2.0 * np.pi * (n * k % count) / count
                total = total + times_phase(rows[n], float(np.cos(angle)), float(np.sin(angle)))
            result.append(total)
        return result
    even, odd = short_dft(rows[0::2]), short_dft(rows[1::2])
    half = count // 2
    low, high = [], []
    for k in range(half):
        if k == 0:
            turned = odd[k]
        elif 4 * k == count:
            turned = times_minus_i(odd[k])
        else:
            angle = 2.0 * np.pi * k / count
            turned = times_phase(odd[k], float(np.cos(angle)), float(np.sin(angle)))
        low.append(even[k] + turned)
        high.append(even[k] - turned)
    return low + high


def twisted(row, twist, full, tail):
    along, across = twist[0:1, :], twist[1:2, :]
    tail_values = row.tail
    if tail_values is not None:
        tail_values = tail_values * along[:, 2 * full :] + swapped(tail_values) * across[:, 2 * full :]
    return Row(
        row.re * along[:, :full] + row.im * across[:, :full],
        row.im * along[:, :full] + row.re * across[:, full : 2 * full],
        tail_values,
    )


def times_conj(ref, sec):
    tail = None
    if ref.tail is not None:
        straight = ref.tail * sec.tail
        crossed = ref.tail * swapped(sec.tail)
        tail = jnp.where(
            first_half(straight), straight + swapped(straight), crossed - swapped(crossed)
        )
    return Row(
        ref.re * sec.re + ref.im * sec.im,
        ref.im * sec.re - ref.re * sec.im,
        tail,
    )


def kernel(
    slc_ref, inner_hbm, twist_hbm, bins_hbm, pool_hbm, start_hbm, stop_hbm, out_ref,
    raw, packed, inner, twist_ref, bins_ref, pool_ref, start_ref, stop_ref, gathered, spectrum, partner, looked, landed,
    load_sem, table_sem, in_send, in_recv, date_send, date_recv, out_send, out_recv,
):
    outer = lax.axis_size("line")
    dates = lax.axis_size("date")
    me = lax.axis_index("line")
    date = lax.axis_index("date")
    width, columns_all = raw.shape[1], raw.shape[2]
    columns = columns_all // outer
    sizes = chunk_sizes(columns)
    chunks = len(sizes)
    begins = [sum(sizes[:i]) for i in range(chunks)]
    full, tail, _, _ = layout(width)
    previous = lax.rem(date + dates - 1, dates)
    following = lax.rem(date + 1, dates)

    barrier = pltpu.get_barrier_semaphore()
    for step in range(1, outer):
        pl.semaphore_signal(
            barrier, inc=1, device_id={"line": lax.rem(me + step, outer)}, device_id_type=MESH
        )
    for other in (previous, following):
        pl.semaphore_signal(barrier, inc=1, device_id={"date": other}, device_id_type=MESH)

    load = pltpu.make_async_copy(slc_ref.at[0], raw, load_sem)
    load.start()
    tables_in = [
        pltpu.make_async_copy(source, target, table_sem.at[t])
        for t, (source, target) in enumerate(
            [
                (start_hbm, start_ref),
                (stop_hbm, stop_ref),
                (twist_hbm, twist_ref),
                (bins_hbm, bins_ref),
                (inner_hbm, inner),
                (pool_hbm, pool_ref),
            ]
        )
    ]
    for table in tables_in:
        table.start()
    load.wait()
    packed[:, :full] = raw[0, :full].T
    packed[:, full : 2 * full] = raw[1, :full].T
    if tail:
        packed[:, 2 * full :] = jnp.concatenate([raw[0, full:], raw[1, full:]], axis=0).T
    pl.semaphore_wait(barrier, outer + 1)

    def rows_of(line, i):
        return pl.ds(pl.multiple_of(line * columns + begins[i], 8), sizes[i])

    def part(i):
        return pl.ds(begins[i], sizes[i])

    incoming = {}
    for i in range(chunks):
        for step in range(outer - 1, 0, -1):
            there = lax.rem(me + step, outer)
            incoming[i, step] = pltpu.make_async_remote_copy(
                src_ref=packed.at[rows_of(there, i)],
                dst_ref=gathered.at[me, part(i)],
                send_sem=in_send.at[i, step],
                recv_sem=in_recv.at[i, step],
                device_id={"line": there},
                device_id_type=MESH,
            )
            incoming[i, step].start()
    gathered[me] = packed[pl.ds(pl.multiple_of(me * columns, 8), columns), :]

    for table in tables_in:
        table.wait()
    lower = start_ref[date]
    upper = stop_ref[date]
    bins = bins_ref[...]
    keep = (bins >= lower) & (bins < upper)
    lane = lax.broadcasted_iota(jnp.int32, bins.shape, 2)
    imaginary = ((lane >= full) & (lane < 2 * full)) | (lane >= 2 * full + tail)
    keep_conj = jnp.where(keep, jnp.where(imaginary, -1.0, 1.0), 0.0).astype(jnp.float32)

    def inner_dft(values):
        high, low = split(values)
        dot = functools.partial(jnp.dot, preferred_element_type=jnp.float32)
        return dot(high, inner[0]) + (dot(low, inner[0]) + dot(high, inner[1]))

    samples = width // LOOKS
    lines_all = outer * width
    out_lane = lax.broadcasted_iota(jnp.int32, (1, 2 * samples), 1)
    scale = 1.0 / (lines_all * lines_all * LOOKS)
    out_scale = jnp.where(out_lane < samples, scale, -scale).astype(jnp.float32)

    handed, outgoing = {}, {}

    def forward(i):
        for step in range(1, outer):
            incoming[i, step].wait_recv()
        rows = short_dft([as_row(gathered[l, part(i), :], full, tail) for l in range(outer)])
        rows = [rows[0]] + [twisted(rows[k], twist_ref[k], full, tail) for k in range(1, outer)]
        result = inner_dft(jnp.concatenate([row.flat() for row in rows], axis=0))
        spectrum[:, part(i), :] = result.reshape(outer, sizes[i], 2 * width)
        handed[i] = pltpu.make_async_remote_copy(
            src_ref=spectrum.at[:, part(i)],
            dst_ref=partner.at[:, part(i)],
            send_sem=date_send.at[i],
            recv_sem=date_recv.at[i],
            device_id={"date": previous},
            device_id_type=MESH,
        )
        handed[i].start()

    def signal(values, chunk):
        rows = []
        for k in range(outer):
            row = as_row(values[k * chunk : (k + 1) * chunk], full, tail)
            rows.append(twisted(row, twist_ref[k], full, tail) if k else row)
        return short_dft(rows)

    def backward(i):
        handed[i].wait_recv()
        chunk = sizes[i]
        both = jnp.concatenate(
            [spectrum[:, part(i), :] * keep_conj, partner[:, part(i), :] * keep_conj], axis=0
        )
        both = inner_dft(both.reshape(2 * outer * chunk, 2 * width))
        ref = signal(both[: outer * chunk], chunk)
        sec = signal(both[outer * chunk :], chunk)
        product = jnp.concatenate([times_conj(r, s).flat() for r, s in zip(ref, sec)], axis=0)
        high, low = split(product)
        weights = pool_ref[...]
        means = jnp.dot(high, weights, preferred_element_type=jnp.float32)
        means = (means + jnp.dot(low, weights, preferred_element_type=jnp.float32)) * out_scale
        looked[:, part(i), :] = means.reshape(outer, chunk, 2 * samples)
        for step in range(1, outer):
            there = lax.rem(me + step, outer)
            outgoing[i, step] = pltpu.make_async_remote_copy(
                src_ref=looked.at[there, part(i)],
                dst_ref=landed.at[rows_of(me, i)],
                send_sem=out_send.at[i, step],
                recv_sem=out_recv.at[i, step],
                device_id={"line": there},
                device_id_type=MESH,
            )
            outgoing[i, step].start()
        landed[rows_of(me, i), :] = looked[me, part(i), :]

    for i in range(chunks + 1):
        if i < chunks:
            forward(i)
        if i >= 1:
            backward(i - 1)

    for copy in outgoing.values():
        copy.wait_recv()
    out_ref[0] = landed[...].T.reshape(2, samples, columns_all)
    for copies in (incoming, handed, outgoing):
        for copy in copies.values():
            copy.wait_send()


def shards(slc, band_start, band_stop):
    outer = lax.axis_size("line")
    _, _, columns_all, width = slc.shape
    columns = columns_all // outer
    chunks = len(chunk_sizes(columns))
    samples = width // LOOKS
    inner, twist, bins, pool = (jnp.asarray(t) for t in tables(outer, width))
    vmem = pl.BlockSpec(memory_space=pltpu.VMEM)
    hbm = pl.BlockSpec(memory_space=pltpu.HBM)
    f32 = jnp.float32
    dma = pltpu.SemaphoreType.DMA
    result = pl.pallas_call(
        kernel,
        out_shape=jax.ShapeDtypeStruct((1, 2, samples, columns_all), f32),
        in_specs=[hbm, hbm, hbm, hbm, hbm, hbm, hbm],
        out_specs=vmem,
        scratch_shapes=[
            pltpu.VMEM((2, width, columns_all), f32),
            pltpu.VMEM((columns_all, 2 * width), f32),
            pltpu.VMEM(inner.shape, jnp.bfloat16),
            pltpu.VMEM(twist.shape, f32),
            pltpu.VMEM(bins.shape, jnp.int32),
            pltpu.VMEM(pool.shape, jnp.bfloat16),
            pltpu.SMEM(band_start.shape, jnp.int32),
            pltpu.SMEM(band_stop.shape, jnp.int32),
            pltpu.VMEM((outer, columns, 2 * width), f32),
            pltpu.VMEM((outer, columns, 2 * width), f32),
            pltpu.VMEM((outer, columns, 2 * width), f32),
            pltpu.VMEM((outer, columns, 2 * samples), f32),
            pltpu.VMEM((columns_all, 2 * samples), f32),
            dma,
            dma((6,)),
            dma((chunks, outer)),
            dma((chunks, outer)),
            dma((chunks,)),
            dma((chunks,)),
            dma((chunks, outer)),
            dma((chunks, outer)),
        ],
        compiler_params=pltpu.CompilerParams(
            collective_id=0, has_side_effects=True, vmem_limit_bytes=67043328
        ),
    )(jnp.swapaxes(slc, 2, 3), inner, twist, bins, pool, band_start, band_stop)
    return jnp.swapaxes(result, 2, 3)


def solution(mesh):
    return jax.shard_map(
        shards,
        mesh=mesh,
        in_specs=(P("date", None, "stack", "line"), P(), P()),
        out_specs=P("date", None, "stack", "line"),
        check_vma=False,
    )
```

profile of v0, /device:TPU:0, one launch (start us, length us, event | category | flops | bytes accessed | tf_op | source)
XLA Modules:
  0.0 32.7 jit_solution(7434259093319456726)
XLA Ops:
  0.0 31.1 %shard_map.73 = f32[1,2,64,256]{3,2,1,0:T(8,128)} custom-call(f32[1,2,320,256]{3,2,1,0:T(8,128)} %bitcast.2, bf16[2,640,640]{2,1,0:T(8,128)(2,1)} %constant.8.clone.inner_hbm, f32[4,2,640]{2,1,0:T(2,128)} %constant.9.clone.twist_hbm, s32[4,1,640]{2,1,0:T(1,128)} %constant.10.clone.bins_hbm, bf16[640,128]{1,0:T(8,128)(2,1)} %constant.11.clone.pool_hbm, ...), custom_call_target="tpu_custom_call" | custom-call | tf_op jit(solution)/shard_map/pallas_call | solution.py:338
  31.1 1.6 %copy.9 = f32[1,2,256,64]{2,3,1,0:T(8,128)} copy(f32[1,2,256,64]{2,3,1,0:T(8,128)} %bitcast.3) | data formatting | bytes 262144
where the time goes:
time: 32.9 us; the launch traced here: 32.7 us
  Pallas kernels  31.1 us (95%)
  local copies, waits for them, and re-layouts  1.57 us (5%)
    pallas_call x1, Pallas kernels, shards(): pl.pallas_call(kernel, out_shape=jax.ShapeDtypeStruct((1, 2, samples, col...  31.1 us
    unnamed x1, local copies, waits for them, and re-layouts  1.57 us

commit v1 on v0

--- a/solution.py
+++ b/solution.py
@@ -337,7 +337,7 @@
     dma = pltpu.SemaphoreType.DMA
     result = pl.pallas_call(
         kernel,
-        out_shape=jax.ShapeDtypeStruct((1, 2, samples, columns_all), f32),
+        out_shape=pltpu.VMEM((1, 2, samples, columns_all), f32),
         in_specs=[hbm, hbm, hbm, hbm, hbm, hbm, hbm],
         out_specs=vmem,
         scratch_shapes=[
@@ -364,7 +364,7 @@
             dma((chunks, outer)),
         ],
         compiler_params=pltpu.CompilerParams(
-            collective_id=0, has_side_effects=True, vmem_limit_bytes=67043328
+            collective_id=0, has_side_effects=True, vmem_limit_bytes=66000000
         ),
     )(jnp.swapaxes(slc, 2, 3), inner, twist, bins, pool, band_start, band_stop)
     return jnp.swapaxes(result, 2, 3)

time: 32.9 us -> 31.3 us (0.951)
  local copies, waits for them, and re-layouts: 1.57 us -> 0.66 us
  Pallas kernels: 31.1 us -> 30.5 us
    unnamed x1, local copies, waits for them, and re-layouts: 1.57 us -> 0.66 us
    pallas_call x1, Pallas kernels: 31.1 us -> 30.5 us  [shards(): pl.pallas_call(kernel, out_shape=pltpu.VMEM((1, 2, samples, columns_all),...]
where the time goes in v1:
time: 31.3 us; the launch traced here: 31.2 us
  Pallas kernels  30.5 us (97%)
  local copies, waits for them, and re-layouts  0.66 us (2%)
    pallas_call x1, Pallas kernels, shards(): pl.pallas_call(kernel, out_shape=pltpu.VMEM((1, 2, samples, columns_all),...  30.5 us
    unnamed x1, local copies, waits for them, and re-layouts  0.66 us

profile of v1, /device:TPU:0, one launch (start us, length us, event | category | flops | bytes accessed | tf_op | source)
XLA Modules:
  0.0 31.2 jit_solution(16889478126330479380)
XLA Ops:
  0.0 30.5 %shard_map.73 = f32[1,2,64,256]{3,2,1,0:T(8,128)S(1)} custom-call(f32[1,2,320,256]{3,2,1,0:T(8,128)} %bitcast.3, bf16[2,640,640]{2,1,0:T(8,128)(2,1)} %constant.8.clone.inner_hbm, f32[4,2,640]{2,1,0:T(2,128)} %constant.9.clone.twist_hbm, s32[4,1,640]{2,1,0:T(1,128)} %constant.10.clone.bins_hbm, bf16[640,128]{1,0:T(8,128)(2,1)} %constant.11.clone.pool_hbm, ...), custom_call_target="tpu_custom_call" | custom-call | tf_op jit(solution)/shard_map/pallas_call | solution.py:338
  30.5 0.7 %copy.9 = f32[1,2,256,64]{2,3,1,0:T(8,128)} copy(f32[1,2,256,64]{2,3,1,0:T(8,128)S(1)} %bitcast.2) | data formatting | bytes 262144

commit v2 on v1

--- a/solution.py
+++ b/solution.py
@@ -370,9 +370,261 @@
     return jnp.swapaxes(result, 2, 3)
 
 
+def shared_kernel(
+    slc_ref, inner_hbm, twist_hbm, bins_hbm, pool_hbm, start_hbm, stop_hbm, out_ref,
+    raw, packed, inner, twist_ref, bins_ref, pool_ref, start_ref, stop_ref, gathered, ref_signal, sec_signal, looked, landed,
+    load_sem, table_sem, in_send, in_recv, out_send, out_recv,
+):
+    outer = lax.axis_size("line")
+    dates = lax.axis_size("date")
+    me = lax.axis_index("line")
+    date = lax.axis_index("date")
+    width, columns_all = raw.shape[1], raw.shape[2]
+    columns = columns_all // (outer * dates)
+    full, tail, _, _ = layout(width)
+    slots = slot_dates(dates)
+    steps = line_steps(outer)
+
+    def at_date(relative):
+        return lax.rem(date + relative, dates)
+
+    def at_line(step):
+        return lax.rem(me + step, outer)
+
+    def device(relative, step):
+        return {"date": at_date(relative), "line": at_line(step)}
+
+    barrier = pltpu.get_barrier_semaphore()
+    for relative in range(dates):
+        for step in range(outer):
+            if relative or step:
+                pl.semaphore_signal(
+                    barrier, inc=1, device_id=device(relative, step), device_id_type=MESH
+                )
+
+    load = pltpu.make_async_copy(slc_ref.at[0], raw, load_sem)
+    load.start()
+    tables_in = [
+        pltpu.make_async_copy(source, target, table_sem.at[t])
+        for t, (source, target) in enumerate(
+            [
+                (start_hbm, start_ref),
+                (stop_hbm, stop_ref),
+                (twist_hbm, twist_ref),
+                (bins_hbm, bins_ref),
+                (inner_hbm, inner),
+                (pool_hbm, pool_ref),
+            ]
+        )
+    ]
+    for table in tables_in:
+        table.start()
+    load.wait()
+    packed[:, :full] = raw[0, :full].T
+    packed[:, full : 2 * full] = raw[1, :full].T
+    if tail:
+        packed[:, 2 * full :] = jnp.concatenate([raw[0, full:], raw[1, full:]], axis=0).T
+    pl.semaphore_wait(barrier, outer * dates - 1)
+
+    def rows_of(at, line, begin, size):
+        return pl.ds(pl.multiple_of((at * outer + line) * columns + begin, 8), size)
+
+    last = len(slots) - 1
+
+    def parts(k):
+        return last_parts(columns) if k == last else [(0, columns)]
+
+    incoming = {}
+    for k, relative in enumerate(slots):
+        to = dates - relative if relative else 0
+        for c, (begin, size) in enumerate(parts(k)):
+            for step in steps:
+                if to == 0 and step == 0:
+                    continue
+                incoming[k, c, step] = pltpu.make_async_remote_copy(
+                    src_ref=packed.at[rows_of(at_date(to), at_line(step), begin, size)],
+                    dst_ref=gathered.at[k, me, pl.ds(begin, size)],
+                    send_sem=in_send.at[k, c, step],
+                    recv_sem=in_recv.at[k, c, step],
+                    device_id=device(to, step),
+                    device_id_type=MESH,
+                )
+                incoming[k, c, step].start()
+    gathered[slots.index(0), me] = packed[rows_of(date, me, 0, columns), :]
+
+    for table in tables_in:
+        table.wait()
+    bins = bins_ref[...]
+    lane = lax.broadcasted_iota(jnp.int32, bins.shape, 2)
+    imaginary = ((lane >= full) & (lane < 2 * full)) | (lane >= 2 * full + tail)
+    sign = jnp.where(imaginary, -1.0, 1.0).astype(jnp.float32)
+
+    def keep_conj(relative):
+        pair = at_date(relative)
+        return jnp.where((bins >= start_ref[pair]) & (bins < stop_ref[pair]), sign, 0.0)
+
+    def inner_dft(values):
+        high, low = split(values)
+        count = values.shape[0]
+        both = jnp.dot(jnp.concatenate([high, low], axis=0), inner[0], preferred_element_type=jnp.float32)
+        return both[:count] + (both[count:] + jnp.dot(high, inner[1], preferred_element_type=jnp.float32))
+
+    samples = width // LOOKS
+    lines_all = outer * width
+    out_lane = lax.broadcasted_iota(jnp.int32, (1, 2 * samples), 1)
+    scale = 1.0 / (lines_all * lines_all * LOOKS)
+    out_scale = jnp.where(out_lane < samples, scale, -scale).astype(jnp.float32)
+
+    def filtered(k, c):
+        relative = slots[k]
+        before = (relative + dates - 1) % dates
+        begin, size = parts(k)[c]
+        rows = pl.ds(begin, size)
+        lines = short_dft([as_row(gathered[k, l, rows, :], full, tail) for l in range(outer)])
+        lines = [lines[0]] + [twisted(lines[n], twist_ref[n], full, tail) for n in range(1, outer)]
+        spectrum = inner_dft(jnp.concatenate([line.flat() for line in lines], axis=0))
+        spectrum = spectrum.reshape(outer, size, 2 * width)
+        both = jnp.concatenate([spectrum * keep_conj(relative), spectrum * keep_conj(before)], axis=0)
+        both = inner_dft(both.reshape(2 * outer * size, 2 * width)).reshape(2 * outer, size, 2 * width)
+        for base, target, pair in ((0, ref_signal, relative), (outer, sec_signal, before)):
+            lines = []
+            for n in range(outer):
+                line = as_row(both[base + n], full, tail)
+                lines.append(twisted(line, twist_ref[n], full, tail) if n else line)
+            for n, line in enumerate(short_dft(lines)):
+                target[pair, n, rows, :] = line.flat()
+
+    def multilook(pair, begin, size):
+        rows = pl.ds(begin, size)
+        product = [
+            times_conj(
+                as_row(ref_signal[pair, n, rows, :], full, tail),
+                as_row(sec_signal[pair, n, rows, :], full, tail),
+            ).flat()
+            for n in range(outer)
+        ]
+        high, low = split(jnp.concatenate(product, axis=0))
+        means = jnp.dot(jnp.concatenate([high, low], axis=0), pool_ref[...], preferred_element_type=jnp.float32)
+        means = (means[: outer * size] + means[outer * size :]) * out_scale
+        looked[pair, :, rows, :] = means.reshape(outer, size, 2 * samples)
+
+    outgoing = {}
+
+    def send_out(pair, c, begin, size):
+        for step in steps:
+            if pair == 0 and step == 0:
+                landed[rows_of(date, me, begin, size), :] = looked[0, me, pl.ds(begin, size), :]
+                continue
+            outgoing[pair, c, step] = pltpu.make_async_remote_copy(
+                src_ref=looked.at[pair, at_line(step), pl.ds(begin, size)],
+                dst_ref=landed.at[rows_of(date, me, begin, size)],
+                send_sem=out_send.at[pair, c, step],
+                recv_sem=out_recv.at[pair, c, step],
+                device_id=device(pair, step),
+                device_id_type=MESH,
+            )
+            outgoing[pair, c, step].start()
+
+    def ready(k):
+        have = slots[: k + 1]
+        return [
+            p for p in (slots[k], (slots[k] + dates - 1) % dates)
+            if p in have and (p + 1) % dates in have
+        ]
+
+    held = []
+    for k in range(len(slots)):
+        for c, (begin, size) in enumerate(parts(k)):
+            for step in steps:
+                if (k, c, step) in incoming:
+                    incoming[k, c, step].wait_recv()
+            if k == last and c == len(parts(k)) - 1:
+                for args in held:
+                    send_out(*args)
+                held = []
+            filtered(k, c)
+            done = sorted(set(ready(k)), key=lambda p: p == 0)
+            for pair in done:
+                multilook(pair, begin, size)
+                held.append((pair, c, begin, size))
+                if k == last and c == len(parts(k)) - 1:
+                    send_out(*held.pop())
+
+    for copy in outgoing.values():
+        copy.wait_recv()
+    out_ref[0] = landed[...].T.reshape(2, samples, columns_all)
+    for copies in (incoming, outgoing):
+        for copy in copies.values():
+            copy.wait_send()
+
+
+def slot_dates(dates):
+    return list(range(1, dates, 2)) + list(range(2, dates, 2)) + [0]
+
+
+def line_steps(outer):
+    return sorted(range(outer), key=lambda step: (abs(2 * step - outer), step))
+
+
+def last_parts(columns):
+    half = columns // 2
+    return [(0, columns)] if columns % 16 else [(0, half), (half, half)]
+
+
+def shared_shards(slc, band_start, band_stop):
+    outer = lax.axis_size("line")
+    dates = lax.axis_size("date")
+    _, _, columns_all, width = slc.shape
+    columns = columns_all // (outer * dates)
+    samples = width // LOOKS
+    inner, twist, bins, pool = (jnp.asarray(t) for t in tables(outer, width))
+    vmem = pl.BlockSpec(memory_space=pltpu.VMEM)
+    hbm = pl.BlockSpec(memory_space=pltpu.HBM)
+    f32 = jnp.float32
+    dma = pltpu.SemaphoreType.DMA
+    most = len(last_parts(columns))
+    result = pl.pallas_call(
+        shared_kernel,
+        out_shape=pltpu.VMEM((1, 2, samples, columns_all), f32),
+        in_specs=[hbm, hbm, hbm, hbm, hbm, hbm, hbm],
+        out_specs=vmem,
+        scratch_shapes=[
+            pltpu.VMEM((2, width, columns_all), f32),
+            pltpu.VMEM((columns_all, 2 * width), f32),
+            pltpu.VMEM(inner.shape, jnp.bfloat16),
+            pltpu.VMEM(twist.shape, f32),
+            pltpu.VMEM(bins.shape, jnp.int32),
+            pltpu.VMEM(pool.shape, jnp.bfloat16),
+            pltpu.SMEM(band_start.shape, jnp.int32),
+            pltpu.SMEM(band_stop.shape, jnp.int32),
+            pltpu.VMEM((dates, outer, columns, 2 * width), f32),
+            pltpu.VMEM((dates, outer, columns, 2 * width), f32),
+            pltpu.VMEM((dates, outer, columns, 2 * width), f32),
+            pltpu.VMEM((dates, outer, columns, 2 * samples), f32),
+            pltpu.VMEM((columns_all, 2 * samples), f32),
+            dma,
+            dma((6,)),
+            dma((dates, most, outer)),
+            dma((dates, most, outer)),
+            dma((dates, most, outer)),
+            dma((dates, most, outer)),
+        ],
+        compiler_params=pltpu.CompilerParams(
+            collective_id=0, has_side_effects=True, vmem_limit_bytes=66000000
+        ),
+    )(jnp.swapaxes(slc, 2, 3), inner, twist, bins, pool, band_start, band_stop)
+    return jnp.swapaxes(result, 2, 3)
+
+
 def solution(mesh):
+    group = mesh.shape["line"] * mesh.shape["date"]
+
+    def body(slc, band_start, band_stop):
+        shared = mesh.shape["date"] > 1 and slc.shape[2] % (8 * group) == 0
+        return (shared_shards if shared else shards)(slc, band_start, band_stop)
+
     return jax.shard_map(
-        shards,
+        body,
         mesh=mesh,
         in_specs=(P("date", None, "stack", "line"), P(), P()),
         out_specs=P("date", None, "stack", "line"),

time: 31.3 us -> 30.2 us (0.965)
  Pallas kernels: 30.5 us -> 29.3 us
    pallas_call x1, Pallas kernels: 30.5 us -> 29.3 us  [shared_shards(): pl.pallas_call(shared_kernel, out_shape=pltpu.VMEM((1, 2, samples, column...]
where the time goes in v2:
time: 30.2 us; the launch traced here: 30 us
  Pallas kernels  29.3 us (97%)
  local copies, waits for them, and re-layouts  0.66 us (2%)
    pallas_call x1, Pallas kernels, shared_shards(): pl.pallas_call(shared_kernel, out_shape=pltpu.VMEM((1, 2, samples, column...  29.3 us
    unnamed x1, local copies, waits for them, and re-layouts  0.66 us

profile of v2, /device:TPU:0, one launch (start us, length us, event | category | flops | bytes accessed | tf_op | source)
XLA Modules:
  0.0 30.0 jit_solution(13092902670640110480)
XLA Ops:
  0.0 29.3 %shard_map.73 = f32[1,2,64,256]{3,2,1,0:T(8,128)S(1)} custom-call(f32[1,2,320,256]{3,2,1,0:T(8,128)} %bitcast.3, bf16[2,640,640]{2,1,0:T(8,128)(2,1)} %constant.8.clone.inner_hbm, f32[4,2,640]{2,1,0:T(2,128)} %constant.9.clone.twist_hbm, s32[4,1,640]{2,1,0:T(1,128)} %constant.10.clone.bins_hbm, bf16[640,128]{1,0:T(8,128)(2,1)} %constant.11.clone.pool_hbm, ...), custom_call_target="tpu_custom_call" | custom-call | tf_op jit(solution)/shard_map/pallas_call | solution.py:586
  29.3 0.7 %copy.9 = f32[1,2,256,64]{2,3,1,0:T(8,128)} copy(f32[1,2,256,64]{2,3,1,0:T(8,128)S(1)} %bitcast.2) | data formatting | bytes 262144

commit v3 on v2

--- a/solution.py
+++ b/solution.py
@@ -383,8 +383,6 @@
     columns = columns_all // (outer * dates)
     full, tail, _, _ = layout(width)
     slots = slot_dates(dates)
-    steps = line_steps(outer)
-
     def at_date(relative):
         return lax.rem(date + relative, dates)
 
@@ -424,33 +422,27 @@
     packed[:, full : 2 * full] = raw[1, :full].T
     if tail:
         packed[:, 2 * full :] = jnp.concatenate([raw[0, full:], raw[1, full:]], axis=0).T
+
     pl.semaphore_wait(barrier, outer * dates - 1)
 
-    def rows_of(at, line, begin, size):
-        return pl.ds(pl.multiple_of((at * outer + line) * columns + begin, 8), size)
-
-    last = len(slots) - 1
-
-    def parts(k):
-        return last_parts(columns) if k == last else [(0, columns)]
+    def rows_of(at, line):
+        return pl.ds(pl.multiple_of((at * outer + line) * columns, 8), columns)
 
     incoming = {}
     for k, relative in enumerate(slots):
-        to = dates - relative if relative else 0
-        for c, (begin, size) in enumerate(parts(k)):
-            for step in steps:
-                if to == 0 and step == 0:
-                    continue
-                incoming[k, c, step] = pltpu.make_async_remote_copy(
-                    src_ref=packed.at[rows_of(at_date(to), at_line(step), begin, size)],
-                    dst_ref=gathered.at[k, me, pl.ds(begin, size)],
-                    send_sem=in_send.at[k, c, step],
-                    recv_sem=in_recv.at[k, c, step],
+        to = (dates - relative) % dates
+        for step in range(outer - 1, -1, -1):
+            if to or step:
+                incoming[k, step] = pltpu.make_async_remote_copy(
+                    src_ref=packed.at[rows_of(at_date(to), at_line(step))],
+                    dst_ref=gathered.at[k, me],
+                    send_sem=in_send.at[k, step],
+                    recv_sem=in_recv.at[k, step],
                     device_id=device(to, step),
                     device_id_type=MESH,
                 )
-                incoming[k, c, step].start()
-    gathered[slots.index(0), me] = packed[rows_of(date, me, 0, columns), :]
+                incoming[k, step].start()
+    gathered[slots.index(0), me] = packed[rows_of(date, me), :]
 
     for table in tables_in:
         table.wait()
@@ -475,80 +467,74 @@
     scale = 1.0 / (lines_all * lines_all * LOOKS)
     out_scale = jnp.where(out_lane < samples, scale, -scale).astype(jnp.float32)
 
-    def filtered(k, c):
+    def filtered(k):
         relative = slots[k]
         before = (relative + dates - 1) % dates
-        begin, size = parts(k)[c]
-        rows = pl.ds(begin, size)
-        lines = short_dft([as_row(gathered[k, l, rows, :], full, tail) for l in range(outer)])
+        lines = short_dft([as_row(gathered[k, l], full, tail) for l in range(outer)])
         lines = [lines[0]] + [twisted(lines[n], twist_ref[n], full, tail) for n in range(1, outer)]
         spectrum = inner_dft(jnp.concatenate([line.flat() for line in lines], axis=0))
-        spectrum = spectrum.reshape(outer, size, 2 * width)
+        spectrum = spectrum.reshape(outer, columns, 2 * width)
         both = jnp.concatenate([spectrum * keep_conj(relative), spectrum * keep_conj(before)], axis=0)
-        both = inner_dft(both.reshape(2 * outer * size, 2 * width)).reshape(2 * outer, size, 2 * width)
+        both = inner_dft(both.reshape(2 * outer * columns, 2 * width))
+        both = both.reshape(2 * outer, columns, 2 * width)
         for base, target, pair in ((0, ref_signal, relative), (outer, sec_signal, before)):
             lines = []
             for n in range(outer):
                 line = as_row(both[base + n], full, tail)
                 lines.append(twisted(line, twist_ref[n], full, tail) if n else line)
             for n, line in enumerate(short_dft(lines)):
-                target[pair, n, rows, :] = line.flat()
-
-    def multilook(pair, begin, size):
-        rows = pl.ds(begin, size)
+                target[pair, n] = line.flat()
+
+    def multilook(pair):
         product = [
             times_conj(
-                as_row(ref_signal[pair, n, rows, :], full, tail),
-                as_row(sec_signal[pair, n, rows, :], full, tail),
+                as_row(ref_signal[pair, n], full, tail), as_row(sec_signal[pair, n], full, tail)
             ).flat()
             for n in range(outer)
         ]
         high, low = split(jnp.concatenate(product, axis=0))
         means = jnp.dot(jnp.concatenate([high, low], axis=0), pool_ref[...], preferred_element_type=jnp.float32)
-        means = (means[: outer * size] + means[outer * size :]) * out_scale
-        looked[pair, :, rows, :] = means.reshape(outer, size, 2 * samples)
+        means = (means[: outer * columns] + means[outer * columns :]) * out_scale
+        looked[pair] = means.reshape(outer, columns, 2 * samples)
 
     outgoing = {}
 
-    def send_out(pair, c, begin, size):
-        for step in steps:
+    def send_out(pair):
+        for step in [*range(1, outer), 0]:
             if pair == 0 and step == 0:
-                landed[rows_of(date, me, begin, size), :] = looked[0, me, pl.ds(begin, size), :]
+                landed[rows_of(date, me), :] = looked[0, me]
                 continue
-            outgoing[pair, c, step] = pltpu.make_async_remote_copy(
-                src_ref=looked.at[pair, at_line(step), pl.ds(begin, size)],
-                dst_ref=landed.at[rows_of(date, me, begin, size)],
-                send_sem=out_send.at[pair, c, step],
-                recv_sem=out_recv.at[pair, c, step],
+            outgoing[pair, step] = pltpu.make_async_remote_copy(
+                src_ref=looked.at[pair, at_line(step)],
+                dst_ref=landed.at[rows_of(date, me)],
+                send_sem=out_send.at[pair, step],
+                recv_sem=out_recv.at[pair, step],
                 device_id=device(pair, step),
                 device_id_type=MESH,
             )
-            outgoing[pair, c, step].start()
+            outgoing[pair, step].start()
 
     def ready(k):
         have = slots[: k + 1]
-        return [
-            p for p in (slots[k], (slots[k] + dates - 1) % dates)
-            if p in have and (p + 1) % dates in have
-        ]
+        pairs = {slots[k], (slots[k] + dates - 1) % dates}
+        return sorted((p for p in pairs if p in have and (p + 1) % dates in have), key=lambda p: p == 0)
 
     held = []
     for k in range(len(slots)):
-        for c, (begin, size) in enumerate(parts(k)):
-            for step in steps:
-                if (k, c, step) in incoming:
-                    incoming[k, c, step].wait_recv()
-            if k == last and c == len(parts(k)) - 1:
-                for args in held:
-                    send_out(*args)
-                held = []
-            filtered(k, c)
-            done = sorted(set(ready(k)), key=lambda p: p == 0)
-            for pair in done:
-                multilook(pair, begin, size)
-                held.append((pair, c, begin, size))
-                if k == last and c == len(parts(k)) - 1:
-                    send_out(*held.pop())
+        for step in range(outer):
+            if (k, step) in incoming:
+                incoming[k, step].wait_recv()
+        final = k == len(slots) - 1
+        if final:
+            for pair in held:
+                send_out(pair)
+        filtered(k)
+        for pair in ready(k):
+            multilook(pair)
+            if final:
+                send_out(pair)
+            else:
+                held.append(pair)
 
     for copy in outgoing.values():
         copy.wait_recv()
@@ -560,15 +546,6 @@
 
 def slot_dates(dates):
     return list(range(1, dates, 2)) + list(range(2, dates, 2)) + [0]
-
-
-def line_steps(outer):
-    return sorted(range(outer), key=lambda step: (abs(2 * step - outer), step))
-
-
-def last_parts(columns):
-    half = columns // 2
-    return [(0, columns)] if columns % 16 else [(0, half), (half, half)]
 
 
 def shared_shards(slc, band_start, band_stop):
@@ -582,7 +559,6 @@
     hbm = pl.BlockSpec(memory_space=pltpu.HBM)
     f32 = jnp.float32
     dma = pltpu.SemaphoreType.DMA
-    most = len(last_parts(columns))
     result = pl.pallas_call(
         shared_kernel,
         out_shape=pltpu.VMEM((1, 2, samples, columns_all), f32),
@@ -604,10 +580,10 @@
             pltpu.VMEM((columns_all, 2 * samples), f32),
             dma,
             dma((6,)),
-            dma((dates, most, outer)),
-            dma((dates, most, outer)),
-            dma((dates, most, outer)),
-            dma((dates, most, outer)),
+            dma((dates, outer)),
+            dma((dates, outer)),
+            dma((dates, outer)),
+            dma((dates, outer)),
         ],
         compiler_params=pltpu.CompilerParams(
             collective_id=0, has_side_effects=True, vmem_limit_bytes=66000000
@@ -620,7 +596,7 @@
     group = mesh.shape["line"] * mesh.shape["date"]
 
     def body(slc, band_start, band_stop):
-        shared = mesh.shape["date"] > 1 and slc.shape[2] % (8 * group) == 0
+        shared = slc.shape[2] % (8 * group) == 0
         return (shared_shards if shared else shards)(slc, band_start, band_stop)
 
     return jax.shard_map(

time: 30.2 us -> 28.7 us (0.950)
  Pallas kernels: 29.3 us -> 27.9 us
    pallas_call x1, Pallas kernels: 29.3 us -> 27.9 us  [shared_shards(): pl.pallas_call(shared_kernel, out_shape=pltpu.VMEM((1, 2, samples, column...]
where the time goes in v3:
time: 28.7 us; the launch traced here: 28.6 us
  Pallas kernels  27.9 us (97%)
  local copies, waits for them, and re-layouts  0.66 us (2%)
    pallas_call x1, Pallas kernels, shared_shards(): pl.pallas_call(shared_kernel, out_shape=pltpu.VMEM((1, 2, samples, column...  27.9 us
    unnamed x1, local copies, waits for them, and re-layouts  0.66 us

profile of v3, /device:TPU:0, one launch (start us, length us, event | category | flops | bytes accessed | tf_op | source)
XLA Modules:
  0.0 28.6 jit_solution(10960893222003216019)
XLA Ops:
  0.0 27.9 %shard_map.73 = f32[1,2,64,256]{3,2,1,0:T(8,128)S(1)} custom-call(f32[1,2,320,256]{3,2,1,0:T(8,128)} %bitcast.3, bf16[2,640,640]{2,1,0:T(8,128)(2,1)} %constant.8.clone.inner_hbm, f32[4,2,640]{2,1,0:T(2,128)} %constant.9.clone.twist_hbm, s32[4,1,640]{2,1,0:T(1,128)} %constant.10.clone.bins_hbm, bf16[640,128]{1,0:T(8,128)(2,1)} %constant.11.clone.pool_hbm, ...), custom_call_target="tpu_custom_call" | custom-call | tf_op jit(solution)/shard_map/pallas_call | solution.py:562
  27.9 0.7 %copy.9 = f32[1,2,256,64]{2,3,1,0:T(8,128)} copy(f32[1,2,256,64]{2,3,1,0:T(8,128)S(1)} %bitcast.2) | data formatting | bytes 262144

commit v4 on v3

--- a/solution.py
+++ b/solution.py
@@ -373,7 +373,7 @@
 def shared_kernel(
     slc_ref, inner_hbm, twist_hbm, bins_hbm, pool_hbm, start_hbm, stop_hbm, out_ref,
     raw, packed, inner, twist_ref, bins_ref, pool_ref, start_ref, stop_ref, gathered, ref_signal, sec_signal, looked, landed,
-    load_sem, table_sem, in_send, in_recv, out_send, out_recv,
+    load_sem, table_sem, in_send, in_recv, out_send, out_recv, from_below, from_above,
 ):
     outer = lax.axis_size("line")
     dates = lax.axis_size("date")
@@ -389,19 +389,60 @@
     def at_line(step):
         return lax.rem(me + step, outer)
 
+    odd = lax.rem(date, 2)
+
+    def slot_date(k):
+        if k > 1 or dates == 2:
+            return slots[k]
+        return slots[k] + odd * (slots[1 - k] - slots[k])
+
     def device(relative, step):
         return {"date": at_date(relative), "line": at_line(step)}
 
+    lower = me < outer // 2
+    upper = me >= outer // 2
+    partner = slot_date(0)
+
     barrier = pltpu.get_barrier_semaphore()
-    for relative in range(dates):
-        for step in range(outer):
-            if relative or step:
+    for near, step in ((me > 0, outer - 1), (me < outer - 1, 1)):
+
+        @pl.when(near)
+        def _():
+            for relative in (0, partner):
                 pl.semaphore_signal(
                     barrier, inc=1, device_id=device(relative, step), device_id_type=MESH
                 )
 
+    for relative in range(1, dates):
+        pl.semaphore_signal(barrier, inc=1, device_id=device(relative, 0), device_id_type=MESH)
+
+    def tell(stage):
+        @pl.when((me > 0) & (me + stage < outer))
+        def _():
+            pl.semaphore_signal(
+                from_above.at[stage], inc=1, device_id={"line": me - 1}, device_id_type=MESH
+            )
+
+        @pl.when((me < outer - 1) & (me >= stage))
+        def _():
+            pl.semaphore_signal(
+                from_below.at[stage], inc=1, device_id={"line": me + 1}, device_id_type=MESH
+            )
+
+    def hear(stage):
+        @pl.when(me + stage + 1 < outer)
+        def _():
+            pl.semaphore_wait(from_above.at[stage], 1)
+
+        @pl.when(me >= stage + 1)
+        def _():
+            pl.semaphore_wait(from_below.at[stage], 1)
+
     load = pltpu.make_async_copy(slc_ref.at[0], raw, load_sem)
     load.start()
+    sides = (me > 0).astype(jnp.int32) + (me < outer - 1).astype(jnp.int32)
+    pl.semaphore_wait(barrier, dates - 1 + 2 * sides)
+    tell(0)
     tables_in = [
         pltpu.make_async_copy(source, target, table_sem.at[t])
         for t, (source, target) in enumerate(
@@ -415,24 +456,23 @@
             ]
         )
     ]
+    load.wait()
     for table in tables_in:
         table.start()
-    load.wait()
     packed[:, :full] = raw[0, :full].T
     packed[:, full : 2 * full] = raw[1, :full].T
     if tail:
         packed[:, 2 * full :] = jnp.concatenate([raw[0, full:], raw[1, full:]], axis=0).T
 
-    pl.semaphore_wait(barrier, outer * dates - 1)
 
     def rows_of(at, line):
         return pl.ds(pl.multiple_of((at * outer + line) * columns, 8), columns)
 
     incoming = {}
-    for k, relative in enumerate(slots):
-        to = (dates - relative) % dates
-        for step in range(outer - 1, -1, -1):
-            if to or step:
+    for k in range(len(slots)):
+        to = slot_date(k) if k < 2 else (dates - slots[k]) % dates
+        for step in range(outer):
+            if slots[k] or step:
                 incoming[k, step] = pltpu.make_async_remote_copy(
                     src_ref=packed.at[rows_of(at_date(to), at_line(step))],
                     dst_ref=gathered.at[k, me],
@@ -441,7 +481,41 @@
                     device_id=device(to, step),
                     device_id_type=MESH,
                 )
-                incoming[k, step].start()
+
+    sent = {}
+
+    def send_in(k, step, known):
+        if (k, step) not in incoming:
+            return
+        before = sent.get((k, step))
+        sent[k, step] = known if before is None or known is None else before | known
+        if before is not None:
+            known = jnp.logical_not(before) if known is None else known & jnp.logical_not(before)
+        if known is None:
+            incoming[k, step].start()
+        else:
+            pl.when(known)(incoming[k, step].start)
+
+    def distance(step):
+        there = at_line(step)
+        return jnp.maximum(there - me, me - there)
+
+    def send_known(stage, ks):
+        for k in ks:
+            for step in range(outer - 1, -1, -1):
+                near = stage + 2 if k in (0, len(slots) - 1) else stage + 1
+                send_in(k, step, distance(step) <= near)
+
+    for step, side in ((1, lower), (outer - 1, upper)):
+        send_in(0, step, side)
+    hear(0)
+    send_known(0, [0])
+    for stage in range(1, outer - 1):
+        tell(stage)
+        hear(stage)
+    for k in range(len(slots)):
+        for step in range(outer - 1, -1, -1):
+            send_in(k, step, None)
     gathered[slots.index(0), me] = packed[rows_of(date, me), :]
 
     for table in tables_in:
@@ -468,8 +542,8 @@
     out_scale = jnp.where(out_lane < samples, scale, -scale).astype(jnp.float32)
 
     def filtered(k):
-        relative = slots[k]
-        before = (relative + dates - 1) % dates
+        relative = slot_date(k)
+        before = lax.rem(relative + dates - 1, dates)
         lines = short_dft([as_row(gathered[k, l], full, tail) for l in range(outer)])
         lines = [lines[0]] + [twisted(lines[n], twist_ref[n], full, tail) for n in range(1, outer)]
         spectrum = inner_dft(jnp.concatenate([line.flat() for line in lines], axis=0))
@@ -584,6 +658,8 @@
             dma((dates, outer)),
             dma((dates, outer)),
             dma((dates, outer)),
+            pltpu.SemaphoreType.REGULAR((outer,)),
+            pltpu.SemaphoreType.REGULAR((outer,)),
         ],
         compiler_params=pltpu.CompilerParams(
             collective_id=0, has_side_effects=True, vmem_limit_bytes=66000000
@@ -596,7 +672,7 @@
     group = mesh.shape["line"] * mesh.shape["date"]
 
     def body(slc, band_start, band_stop):
-        shared = slc.shape[2] % (8 * group) == 0
+        shared = slc.shape[2] % (8 * group) == 0 and group > 1 and mesh.shape["date"] % 2 == 0
         return (shared_shards if shared else shards)(slc, band_start, band_stop)
 
     return jax.shard_map(

time: 28.7 us -> 27.9 us (0.972)
  Pallas kernels: 27.9 us -> 27.1 us
    pallas_call x1, Pallas kernels: 27.9 us -> 27.1 us  [shared_shards(): pl.pallas_call(shared_kernel, out_shape=pltpu.VMEM((1, 2, samples, column...]
where the time goes in v4:
time: 27.9 us; the launch traced here: 27.8 us
  Pallas kernels  27.1 us (97%)
  local copies, waits for them, and re-layouts  0.66 us (2%)
    pallas_call x1, Pallas kernels, shared_shards(): pl.pallas_call(shared_kernel, out_shape=pltpu.VMEM((1, 2, samples, column...  27.1 us
    unnamed x1, local copies, waits for them, and re-layouts  0.66 us

profile of v4, /device:TPU:0, one launch (start us, length us, event | category | flops | bytes accessed | tf_op | source)
XLA Modules:
  0.0 27.8 jit_solution(2297276041462596866)
XLA Ops:
  0.0 27.1 %shard_map.73 = f32[1,2,64,256]{3,2,1,0:T(8,128)S(1)} custom-call(f32[1,2,320,256]{3,2,1,0:T(8,128)} %bitcast.3, bf16[2,640,640]{2,1,0:T(8,128)(2,1)} %constant.8.clone.inner_hbm, f32[4,2,640]{2,1,0:T(2,128)} %constant.9.clone.twist_hbm, s32[4,1,640]{2,1,0:T(1,128)} %constant.10.clone.bins_hbm, bf16[640,128]{1,0:T(8,128)(2,1)} %constant.11.clone.pool_hbm, ...), custom_call_target="tpu_custom_call" | custom-call | tf_op jit(solution)/shard_map/pallas_call | solution.py:636
  27.1 0.7 %copy.9 = f32[1,2,256,64]{2,3,1,0:T(8,128)} copy(f32[1,2,256,64]{2,3,1,0:T(8,128)S(1)} %bitcast.2) | data formatting | bytes 262144

commit v5 on v4

--- a/solution.py
+++ b/solution.py
@@ -370,6 +370,77 @@
     return jnp.swapaxes(result, 2, 3)
 
 
+def shared_tables(outer, width):
+    block = LANES // 2
+    lines = outer * width
+    count = lines // block
+    index = np.arange(LANES) % block
+    side = np.arange(LANES) // block
+    angle = 2.0 * np.pi / block * (index[:, None] * index[None, :] % block)
+    same = side[:, None] == side[None, :]
+    dense = np.concatenate([np.where(same, np.cos(angle), 0.0), np.where(same, np.sin(angle), 0.0)], axis=1)
+    dense = dense.astype(np.float32)
+    high = dense.astype(jnp.bfloat16)
+    low = (dense - high.astype(np.float32)).astype(jnp.bfloat16)
+    inner = np.concatenate([high, high, low], axis=0)
+    turn = 2.0 * np.pi / lines * (np.arange(count)[:, None] * index[None, :] % lines)
+    twist = np.stack([np.cos(turn), np.sin(turn)], axis=1).astype(np.float32)
+    bins = (np.arange(count)[:, None] + count * index[None, :]).astype(np.int32)[:, None, :]
+    samples = width // LOOKS
+    line = np.arange(width // block)[:, None, None] * block + np.arange(block)[None, None, :]
+    target = line // LOOKS + samples * np.arange(2)[None, :, None]
+    pool = (target.reshape(-1)[:, None] == np.arange(2 * samples)[None, :]).astype(jnp.bfloat16)
+    return inner, twist, bins, pool
+
+
+def turned(value, c, s):
+    re, im = value
+    return re * c + im * s, im * c - re * s
+
+
+def plus(a, b):
+    return a[0] + b[0], a[1] + b[1]
+
+
+def minus(a, b):
+    return a[0] - b[0], a[1] - b[1]
+
+
+def times(a, factor):
+    return a[0] * factor, a[1] * factor
+
+
+def full_dft(values):
+    count = len(values)
+    if count == 1:
+        return values
+    if count % 2:
+        sums = [plus(values[j], values[count - j]) for j in range(1, count // 2 + 1)]
+        differences = [minus(values[j], values[count - j]) for j in range(1, count // 2 + 1)]
+        result = [None] * count
+        result[0] = functools.reduce(plus, sums, values[0])
+        for k in range(1, count // 2 + 1):
+            angles = [2.0 * np.pi * (j * k % count) / count for j in range(1, count // 2 + 1)]
+            even = functools.reduce(plus, [times(v, float(np.cos(a))) for v, a in zip(sums, angles)], values[0])
+            odd = functools.reduce(plus, [times(v, float(np.sin(a))) for v, a in zip(differences, angles)])
+            result[k] = even[0] + odd[1], even[1] - odd[0]
+            result[count - k] = even[0] - odd[1], even[1] + odd[0]
+        return result
+    even, odd = full_dft(values[0::2]), full_dft(values[1::2])
+    low, high = [], []
+    for k in range(count // 2):
+        if k == 0:
+            moved = odd[k]
+        elif 4 * k == count:
+            moved = odd[k][1], -odd[k][0]
+        else:
+            angle = 2.0 * np.pi * k / count
+            moved = turned(odd[k], float(np.cos(angle)), float(np.sin(angle)))
+        low.append(plus(even[k], moved))
+        high.append(minus(even[k], moved))
+    return low + high
+
+
 def shared_kernel(
     slc_ref, inner_hbm, twist_hbm, bins_hbm, pool_hbm, start_hbm, stop_hbm, out_ref,
     raw, packed, inner, twist_ref, bins_ref, pool_ref, start_ref, stop_ref, gathered, ref_signal, sec_signal, looked, landed,
@@ -380,8 +451,12 @@
     me = lax.axis_index("line")
     date = lax.axis_index("date")
     width, columns_all = raw.shape[1], raw.shape[2]
-    columns = columns_all // (outer * dates)
-    full, tail, _, _ = layout(width)
+    half = columns_all // 2
+    rows = half // (outer * dates)
+    block = LANES // 2
+    blocks = width // block
+    count = outer * blocks
+    flat = 2 * width
     slots = slot_dates(dates)
     def at_date(relative):
         return lax.rem(date + relative, dates)
@@ -459,14 +534,14 @@
     load.wait()
     for table in tables_in:
         table.start()
-    packed[:, :full] = raw[0, :full].T
-    packed[:, full : 2 * full] = raw[1, :full].T
-    if tail:
-        packed[:, 2 * full :] = jnp.concatenate([raw[0, full:], raw[1, full:]], axis=0).T
-
+    for part in range(2):
+        for n in range(blocks):
+            lines = raw[part, n * block : (n + 1) * block]
+            both = jnp.concatenate([lines[:, :half], lines[:, half:]], axis=0)
+            packed[:, part * flat + n * LANES : part * flat + (n + 1) * LANES] = both.T
 
     def rows_of(at, line):
-        return pl.ds(pl.multiple_of((at * outer + line) * columns, 8), columns)
+        return pl.ds(pl.multiple_of((at * outer + line) * rows, 8), rows)
 
     incoming = {}
     for k in range(len(slots)):
@@ -521,55 +596,75 @@
     for table in tables_in:
         table.wait()
     bins = bins_ref[...]
-    lane = lax.broadcasted_iota(jnp.int32, bins.shape, 2)
-    imaginary = ((lane >= full) & (lane < 2 * full)) | (lane >= 2 * full + tail)
-    sign = jnp.where(imaginary, -1.0, 1.0).astype(jnp.float32)
-
-    def keep_conj(relative):
+
+    def kept(relative):
         pair = at_date(relative)
-        return jnp.where((bins >= start_ref[pair]) & (bins < stop_ref[pair]), sign, 0.0)
-
-    def inner_dft(values):
+        return jnp.where((bins >= start_ref[pair]) & (bins < stop_ref[pair]), 1.0, 0.0).astype(jnp.float32)
+
+    def inner_dft(re, im):
+        values = jnp.concatenate([re, im], axis=0)
         high, low = split(values)
-        count = values.shape[0]
-        both = jnp.dot(jnp.concatenate([high, low], axis=0), inner[0], preferred_element_type=jnp.float32)
-        return both[:count] + (both[count:] + jnp.dot(high, inner[1], preferred_element_type=jnp.float32))
+        both = jnp.dot(
+            jnp.concatenate([high, low, high], axis=1), inner[...], preferred_element_type=jnp.float32
+        )
+        size = re.shape[0]
+        return (
+            both[:size, :LANES] + both[size:, LANES:],
+            both[size:, :LANES] - both[:size, LANES:],
+        )
+
+    def twisted_by(values):
+        return [values[0]] + [
+            turned(values[n], twist_ref[n, 0:1, :], twist_ref[n, 1:2, :]) for n in range(1, len(values))
+        ]
 
     samples = width // LOOKS
     lines_all = outer * width
-    out_lane = lax.broadcasted_iota(jnp.int32, (1, 2 * samples), 1)
     scale = 1.0 / (lines_all * lines_all * LOOKS)
-    out_scale = jnp.where(out_lane < samples, scale, -scale).astype(jnp.float32)
+
+    def lanes(part, n):
+        return slice(part * flat + n * LANES, part * flat + (n + 1) * LANES)
 
     def filtered(k):
         relative = slot_date(k)
         before = lax.rem(relative + dates - 1, dates)
-        lines = short_dft([as_row(gathered[k, l], full, tail) for l in range(outer)])
-        lines = [lines[0]] + [twisted(lines[n], twist_ref[n], full, tail) for n in range(1, outer)]
-        spectrum = inner_dft(jnp.concatenate([line.flat() for line in lines], axis=0))
-        spectrum = spectrum.reshape(outer, columns, 2 * width)
-        both = jnp.concatenate([spectrum * keep_conj(relative), spectrum * keep_conj(before)], axis=0)
-        both = inner_dft(both.reshape(2 * outer * columns, 2 * width))
-        both = both.reshape(2 * outer, columns, 2 * width)
-        for base, target, pair in ((0, ref_signal, relative), (outer, sec_signal, before)):
-            lines = []
-            for n in range(outer):
-                line = as_row(both[base + n], full, tail)
-                lines.append(twisted(line, twist_ref[n], full, tail) if n else line)
-            for n, line in enumerate(short_dft(lines)):
-                target[pair, n] = line.flat()
+        values = [
+            (gathered[k, l, :, lanes(0, n)], gathered[k, l, :, lanes(1, n)])
+            for l in range(outer)
+            for n in range(blocks)
+        ]
+        values = twisted_by(full_dft(values))
+        re, im = inner_dft(
+            jnp.concatenate([v[0] for v in values], axis=0), jnp.concatenate([v[1] for v in values], axis=0)
+        )
+        re, im = re.reshape(count, rows, LANES), im.reshape(count, rows, LANES)
+        keeps = [kept(relative), kept(before)]
+        re = jnp.concatenate([re * keep for keep in keeps], axis=0).reshape(2 * count * rows, LANES)
+        im = jnp.concatenate([im * -keep for keep in keeps], axis=0).reshape(2 * count * rows, LANES)
+        re, im = inner_dft(re, im)
+        for base, target, pair in ((0, ref_signal, relative), (count, sec_signal, before)):
+            values = [
+                (re[(base + n) * rows : (base + n + 1) * rows], im[(base + n) * rows : (base + n + 1) * rows])
+                for n in range(count)
+            ]
+            values = full_dft(twisted_by(values))
+            for n, value in enumerate(values):
+                for part in range(2):
+                    target[pair, n // blocks, :, lanes(part, n % blocks)] = value[part]
 
     def multilook(pair):
-        product = [
-            times_conj(
-                as_row(ref_signal[pair, n], full, tail), as_row(sec_signal[pair, n], full, tail)
-            ).flat()
-            for n in range(outer)
-        ]
-        high, low = split(jnp.concatenate(product, axis=0))
+        re, im = [], []
+        for l in range(outer):
+            ref_re, ref_im = ref_signal[pair, l, :, :flat], ref_signal[pair, l, :, flat:]
+            sec_re, sec_im = sec_signal[pair, l, :, :flat], sec_signal[pair, l, :, flat:]
+            re.append(ref_re * sec_re + ref_im * sec_im)
+            im.append(ref_im * sec_re - ref_re * sec_im)
+        high, low = split(jnp.concatenate(re + im, axis=0))
         means = jnp.dot(jnp.concatenate([high, low], axis=0), pool_ref[...], preferred_element_type=jnp.float32)
-        means = (means[: outer * columns] + means[outer * columns :]) * out_scale
-        looked[pair] = means.reshape(outer, columns, 2 * samples)
+        size = outer * rows
+        means = means[: 2 * size] + means[2 * size :]
+        looked[pair, :, :, : 2 * samples] = (means[:size] * scale).reshape(outer, rows, 2 * samples)
+        looked[pair, :, :, 2 * samples :] = (means[size:] * -scale).reshape(outer, rows, 2 * samples)
 
     outgoing = {}
 
@@ -612,7 +707,10 @@
 
     for copy in outgoing.values():
         copy.wait_recv()
-    out_ref[0] = landed[...].T.reshape(2, samples, columns_all)
+    for part in range(2):
+        turned_back = landed[:, part * 2 * samples : (part + 1) * 2 * samples].T
+        out_ref[0, part, :, :half] = turned_back[:samples]
+        out_ref[0, part, :, half:] = turned_back[samples:]
     for copies in (incoming, outgoing):
         for copy in copies.values():
             copy.wait_send()
@@ -626,9 +724,10 @@
     outer = lax.axis_size("line")
     dates = lax.axis_size("date")
     _, _, columns_all, width = slc.shape
-    columns = columns_all // (outer * dates)
+    half = columns_all // 2
+    rows = half // (outer * dates)
     samples = width // LOOKS
-    inner, twist, bins, pool = (jnp.asarray(t) for t in tables(outer, width))
+    inner, twist, bins, pool = (jnp.asarray(t) for t in shared_tables(outer, width))
     vmem = pl.BlockSpec(memory_space=pltpu.VMEM)
     hbm = pl.BlockSpec(memory_space=pltpu.HBM)
     f32 = jnp.float32
@@ -640,18 +739,18 @@
         out_specs=vmem,
         scratch_shapes=[
             pltpu.VMEM((2, width, columns_all), f32),
-            pltpu.VMEM((columns_all, 2 * width), f32),
+            pltpu.VMEM((half, 4 * width), f32),
             pltpu.VMEM(inner.shape, jnp.bfloat16),
             pltpu.VMEM(twist.shape, f32),
             pltpu.VMEM(bins.shape, jnp.int32),
             pltpu.VMEM(pool.shape, jnp.bfloat16),
             pltpu.SMEM(band_start.shape, jnp.int32),
             pltpu.SMEM(band_stop.shape, jnp.int32),
-            pltpu.VMEM((dates, outer, columns, 2 * width), f32),
-            pltpu.VMEM((dates, outer, columns, 2 * width), f32),
-            pltpu.VMEM((dates, outer, columns, 2 * width), f32),
-            pltpu.VMEM((dates, outer, columns, 2 * samples), f32),
-            pltpu.VMEM((columns_all, 2 * samples), f32),
+            pltpu.VMEM((dates, outer, rows, 4 * width), f32),
+            pltpu.VMEM((dates, outer, rows, 4 * width), f32),
+            pltpu.VMEM((dates, outer, rows, 4 * width), f32),
+            pltpu.VMEM((dates, outer, rows, 4 * samples), f32),
+            pltpu.VMEM((half, 4 * samples), f32),
             dma,
             dma((6,)),
             dma((dates, outer)),
@@ -672,7 +771,9 @@
     group = mesh.shape["line"] * mesh.shape["date"]
 
     def body(slc, band_start, band_stop):
-        shared = slc.shape[2] % (8 * group) == 0 and group > 1 and mesh.shape["date"] % 2 == 0
+        half, width = slc.shape[2] // 2, slc.shape[3]
+        shared = half % (8 * group) == 0 and half % LANES == 0 and mesh.shape["date"] % 2 == 0
+        shared = shared and width % LANES == LANES // 2 and 2 * (width // LOOKS) % LANES == 0
         return (shared_shards if shared else shards)(slc, band_start, band_stop)
 
     return jax.shard_map(

time: 27.9 us -> 27.2 us (0.975)
  Pallas kernels: 27.1 us -> 26.4 us
    pallas_call x1, Pallas kernels: 27.1 us -> 26.4 us  [shared_shards(): pl.pallas_call(shared_kernel, out_shape=pltpu.VMEM((1, 2, samples, column...]
where the time goes in v5:
time: 27.2 us; the launch traced here: 27 us
  Pallas kernels  26.4 us (97%)
  local copies, waits for them, and re-layouts  0.66 us (2%)
    pallas_call x1, Pallas kernels, shared_shards(): pl.pallas_call(shared_kernel, out_shape=pltpu.VMEM((1, 2, samples, column...  26.4 us
    unnamed x1, local copies, waits for them, and re-layouts  0.66 us

profile of v5, /device:TPU:0, one launch (start us, length us, event | category | flops | bytes accessed | tf_op | source)
XLA Modules:
  0.0 27.0 jit_solution(3311636013057167184)
XLA Ops:
  0.0 26.4 %shard_map.73 = f32[1,2,64,256]{3,2,1,0:T(8,128)S(1)} custom-call(f32[1,2,320,256]{3,2,1,0:T(8,128)} %bitcast.3, bf16[384,256]{1,0:T(8,128)(2,1)} %constant.8.clone.inner_hbm, f32[20,2,128]{2,1,0:T(2,128)} %constant.9.clone.twist_hbm, s32[20,1,128]{2,1,0:T(1,128)} %constant.10.clone.bins_hbm, bf16[640,128]{1,0:T(8,128)(2,1)} %constant.11.clone.pool_hbm, ...), custom_call_target="tpu_custom_call" | custom-call | tf_op jit(solution)/shard_map/pallas_call | solution.py:735
  26.4 0.7 %copy.9 = f32[1,2,256,64]{2,3,1,0:T(8,128)} copy(f32[1,2,256,64]{2,3,1,0:T(8,128)S(1)} %bitcast.2) | data formatting | bytes 262144

commit v6 on v5

--- a/solution.py
+++ b/solution.py
@@ -601,6 +601,8 @@
         pair = at_date(relative)
         return jnp.where((bins >= start_ref[pair]) & (bins < stop_ref[pair]), 1.0, 0.0).astype(jnp.float32)
 
+    masks = [kept(relative) for relative in range(dates)]
+
     def inner_dft(re, im):
         values = jnp.concatenate([re, im], axis=0)
         high, low = split(values)
@@ -627,7 +629,7 @@
 
     def filtered(k):
         relative = slot_date(k)
-        before = lax.rem(relative + dates - 1, dates)
+        before = (relative + dates - 1) % dates if k > 1 else lax.rem(relative + dates - 1, dates)
         values = [
             (gathered[k, l, :, lanes(0, n)], gathered[k, l, :, lanes(1, n)])
             for l in range(outer)
@@ -638,7 +640,7 @@
             jnp.concatenate([v[0] for v in values], axis=0), jnp.concatenate([v[1] for v in values], axis=0)
         )
         re, im = re.reshape(count, rows, LANES), im.reshape(count, rows, LANES)
-        keeps = [kept(relative), kept(before)]
+        keeps = [masks[relative], masks[before]] if k > 1 else [kept(relative), kept(before)]
         re = jnp.concatenate([re * keep for keep in keeps], axis=0).reshape(2 * count * rows, LANES)
         im = jnp.concatenate([im * -keep for keep in keeps], axis=0).reshape(2 * count * rows, LANES)
         re, im = inner_dft(re, im)
@@ -652,19 +654,25 @@
                 for part in range(2):
                     target[pair, n // blocks, :, lanes(part, n % blocks)] = value[part]
 
-    def multilook(pair):
+    def multilook(pairs):
+        if not pairs:
+            return
         re, im = [], []
-        for l in range(outer):
-            ref_re, ref_im = ref_signal[pair, l, :, :flat], ref_signal[pair, l, :, flat:]
-            sec_re, sec_im = sec_signal[pair, l, :, :flat], sec_signal[pair, l, :, flat:]
-            re.append(ref_re * sec_re + ref_im * sec_im)
-            im.append(ref_im * sec_re - ref_re * sec_im)
+        for pair in pairs:
+            for l in range(outer):
+                ref_re, ref_im = ref_signal[pair, l, :, :flat], ref_signal[pair, l, :, flat:]
+                sec_re, sec_im = sec_signal[pair, l, :, :flat], sec_signal[pair, l, :, flat:]
+                re.append(ref_re * sec_re + ref_im * sec_im)
+                im.append(ref_im * sec_re - ref_re * sec_im)
         high, low = split(jnp.concatenate(re + im, axis=0))
         means = jnp.dot(jnp.concatenate([high, low], axis=0), pool_ref[...], preferred_element_type=jnp.float32)
         size = outer * rows
-        means = means[: 2 * size] + means[2 * size :]
-        looked[pair, :, :, : 2 * samples] = (means[:size] * scale).reshape(outer, rows, 2 * samples)
-        looked[pair, :, :, 2 * samples :] = (means[size:] * -scale).reshape(outer, rows, 2 * samples)
+        total = size * len(pairs)
+        means = means[: 2 * total] + means[2 * total :]
+        for n, pair in enumerate(pairs):
+            re, im = means[n * size : (n + 1) * size], means[total + n * size : total + (n + 1) * size]
+            looked[pair, :, :, : 2 * samples] = (re * scale).reshape(outer, rows, 2 * samples)
+            looked[pair, :, :, 2 * samples :] = (im * -scale).reshape(outer, rows, 2 * samples)
 
     outgoing = {}
 
@@ -698,8 +706,8 @@
             for pair in held:
                 send_out(pair)
         filtered(k)
+        multilook(ready(k))
         for pair in ready(k):
-            multilook(pair)
             if final:
                 send_out(pair)
             else:

time: 27.2 us -> 27.3 us (level)
  no operation moved by 1% of the time
where the time goes in v6:
time: 27.3 us; the launch traced here: 27.1 us
  Pallas kernels  26.5 us (97%)
  local copies, waits for them, and re-layouts  0.66 us (2%)
    pallas_call x1, Pallas kernels, shared_shards(): pl.pallas_call(shared_kernel, out_shape=pltpu.VMEM((1, 2, samples, column...  26.5 us
    unnamed x1, local copies, waits for them, and re-layouts  0.66 us

profile of v6, /device:TPU:0, one launch (start us, length us, event | category | flops | bytes accessed | tf_op | source)
XLA Modules:
  0.0 27.1 jit_solution(6262547604153934401)
XLA Ops:
  0.0 26.5 %shard_map.73 = f32[1,2,64,256]{3,2,1,0:T(8,128)S(1)} custom-call(f32[1,2,320,256]{3,2,1,0:T(8,128)} %bitcast.3, bf16[384,256]{1,0:T(8,128)(2,1)} %constant.8.clone.inner_hbm, f32[20,2,128]{2,1,0:T(2,128)} %constant.9.clone.twist_hbm, s32[20,1,128]{2,1,0:T(1,128)} %constant.10.clone.bins_hbm, bf16[640,128]{1,0:T(8,128)(2,1)} %constant.11.clone.pool_hbm, ...), custom_call_target="tpu_custom_call" | custom-call | tf_op jit(solution)/shard_map/pallas_call | solution.py:743
  26.5 0.7 %copy.9 = f32[1,2,256,64]{2,3,1,0:T(8,128)} copy(f32[1,2,256,64]{2,3,1,0:T(8,128)S(1)} %bitcast.2) | data formatting | bytes 262144
